TPU v7x, 32 devices: a whole 2x2x4 slice. The times are simulated.
32 devices in a mesh: doc: 4 (over z), term: 8 (over y, x, core).
Axes of the slice: x: 2, y: 2, z: 4, core: 2. Of those that a mesh axis runs over, the one named last changes fastest.
Arguments:
- tiles: bfloat16 [4, 8, 8, 512, 512], P('doc', 'term'), may hold values from 0.0009994507 to 1
- tile_rows: int32 [4, 8, 8], P('doc', 'term'), may hold values from 0 to 31, as said below
- tile_cols: int32 [4, 8, 8], P('doc', 'term'), may hold values from 0 to 63
- counts: int32 [4, 8], P('doc', 'term'), may hold values from 2 to 8, as said below
- start_block: float32 [16, 262144], P(None, 'term'), may hold values from -6 to 6
Outputs:
- left_block: float32 [16, 65536], P(None, ('doc', 'term'))
- right_block: float32 [16, 262144], P(None, ('term', 'doc'))
- coefficients: float32 [5, 16, 16], replicated
Inputs may be any that keep to these rules, and one draw needn't show every extreme that they name: On each device the pairs (tile_rows, tile_cols) of its 8 slots are distinct. `counts`: some device uses all 8 slots.
All inputs are finite; a program needn't handle non-finite values.
Results may differ from a plain program's by a relative error of at most 0.0031.
Values sent between devices are 32-bit elements; how exact they have to be, the bound alone decides.
No kernel may reach another device: no remote copies, remote signals or barrier semaphores. Data moves between devices by JAX's collectives and lax.ppermute only.
A program may use at most 64 MiB of HBM per device.

v0:
```python
import jax
import jax.numpy as jnp
from jax import lax
from jax.sharding import PartitionSpec as P

TERM_TILES = 64
DOC_TILES = 32


def orthonormal(vectors, earlier, total_rows, summed):
    highest = lax.Precision.HIGHEST
    if earlier is None:
        gram_matrix = summed(jnp.dot(vectors, vectors.T, precision=highest) / total_rows)
        factor = jnp.linalg.cholesky(gram_matrix)
        return (jax.scipy.linalg.solve_triangular(factor, vectors, lower=True), factor, None)
    projection, gram_matrix = summed(
        (
            jnp.dot(vectors, earlier.T, precision=highest) / total_rows,
            jnp.dot(vectors, vectors.T, precision=highest) / total_rows,
        )
    )
    gram_matrix = gram_matrix - jnp.dot(projection, projection.T, precision=highest)
    vectors = vectors - jnp.dot(projection, earlier, precision=highest)
    factor = jnp.linalg.cholesky(gram_matrix)
    return (jax.scipy.linalg.solve_triangular(factor, vectors, lower=True), factor, projection)


def on_device(tiles, tile_rows, tile_cols, counts, start_block):
    highest = lax.Precision.HIGHEST
    local_tiles = tiles[0, 0]
    slot_rows = tile_rows[0, 0]
    slot_cols = tile_cols[0, 0]
    in_use = counts[0, 0]
    slot_count = local_tiles.shape[0]
    tile_edge = local_tiles.shape[1]
    block_cols = start_block.shape[0]
    doc_groups = lax.axis_size("doc")
    term_groups = lax.axis_size("term")
    row_count = DOC_TILES * tile_edge
    col_count = TERM_TILES * tile_edge
    n_docs = row_count * doc_groups
    n_terms = col_count * term_groups
    active = (jnp.arange(slot_count) < in_use).astype(jnp.float32)
    row_onehot = (slot_rows[:, None] == jnp.arange(DOC_TILES)[None, :]).astype(jnp.float32)
    col_onehot = (slot_cols[:, None] == jnp.arange(TERM_TILES)[None, :]).astype(jnp.float32)
    row_live = row_onehot * active[:, None]
    col_live = col_onehot * active[:, None]
    ones_edge = jnp.ones((tile_edge,), jnp.bfloat16)
    row_sums = jnp.einsum("kab,b->ka", local_tiles, ones_edge, preferred_element_type=jnp.float32)
    col_sums = jnp.einsum("kab,a->kb", local_tiles, ones_edge, preferred_element_type=jnp.float32)
    row_part = jnp.einsum("kr,ka->ra", row_live, row_sums, precision=highest).reshape(-1)
    col_part = jnp.einsum("kc,kb->cb", col_live, col_sums, precision=highest).reshape(-1)
    row_scale = lax.rsqrt(lax.psum(row_part, "term") + 1.0)
    col_scale = lax.rsqrt(lax.psum(col_part, "doc") + 1.0)
    start_gram = lax.psum(jnp.dot(start_block, start_block.T, precision=highest) / n_terms, "term")
    first_right = jax.scipy.linalg.solve_triangular(
        jnp.linalg.cholesky(start_gram), start_block, lower=True
    )

    def forward(right_block):
        scaled = (
            (right_block * col_scale[None, :])
            .astype(jnp.bfloat16)
            .reshape(block_cols, TERM_TILES, tile_edge)
        )
        pieces = jnp.einsum(
            "kc,bcx->kbx",
            col_onehot.astype(jnp.bfloat16),
            scaled,
            preferred_element_type=jnp.float32,
        ).astype(jnp.bfloat16)
        product = jnp.einsum(
            "kab,kcb->kca", local_tiles, pieces, preferred_element_type=jnp.float32
        )
        return jnp.einsum("kr,kca->cra", row_live, product, precision=highest).reshape(
            block_cols, row_count
        )

    share_rows = row_count // term_groups
    share_cols = col_count // doc_groups

    def doc_total(partial_value):
        return lax.psum(partial_value, "doc")

    def term_total(partial_value):
        return lax.psum(partial_value, "term")

    def doc_side(right_block):
        return lax.psum(forward(right_block), "term") * row_scale[None, :]

    left_one, factor_one, nothing = orthonormal(doc_side(first_right), None, n_docs, doc_total)
    scaled = (
        (left_one * row_scale[None, :])
        .astype(jnp.bfloat16)
        .reshape(block_cols, DOC_TILES, tile_edge)
    )
    pieces = jnp.einsum(
        "kr,brx->kbx", row_onehot.astype(jnp.bfloat16), scaled, preferred_element_type=jnp.float32
    ).astype(jnp.bfloat16)
    product = jnp.einsum("kab,kca->kcb", local_tiles, pieces, preferred_element_type=jnp.float32)
    right_raw = (
        lax.psum(
            jnp.einsum("kc,kxb->xcb", col_live, product, precision=highest).reshape(
                block_cols, col_count
            ),
            "doc",
        )
        * col_scale[None, :]
    )
    right_two, factor_two, projection_one = orthonormal(right_raw, first_right, n_terms, term_total)
    left_two, factor_three, projection_two = orthonormal(
        doc_side(right_two), left_one, n_docs, doc_total
    )
    left_out = lax.dynamic_slice_in_dim(
        left_two, lax.axis_index("term") * share_rows, share_rows, 1
    )
    right_out = lax.dynamic_slice_in_dim(
        right_two, lax.axis_index("doc") * share_cols, share_cols, 1
    )
    coefficients = jnp.stack([factor_one, projection_one, factor_two, projection_two, factor_three])
    return (left_out, right_out, coefficients)


def solution(mesh):
    in_specs = (
        P("doc", "term", None, None, None),
        P("doc", "term", None),
        P("doc", "term", None),
        P("doc", "term"),
        P(None, "term"),
    )
    out_specs = (P(None, ("doc", "term")), P(None, ("term", "doc")), P())
    return jax.shard_map(
        on_device, mesh=mesh, in_specs=in_specs, out_specs=out_specs, check_vma=False
    )
```

profile of v0, /device:TPU:0, one launch (start us, length us, event | category | flops | bytes accessed | tf_op | source)
XLA Modules:
  0.0 372.0 jit_solution(9705424546379850489)
XLA Ops:
  7.2 3.0 fusion.8
  10.9 0.4 convolution_bitcast_fusion
  11.3 0.7 copy.24
  12.0 3.4 fusion.4
  15.4 2.8 convolution_multiply_fusion.3
  18.2 15.8 %psum.77 = f32[16,16]{1,0:T(8,128)S(1)} all-reduce(f32[16,16]{1,0:T(8,128)S(1)} %convolution_multiply_fusion.3), channel_id=1, replica_groups=mesh['doc'=4,'term'=8] {'term'}, use_global_device_ids=true, to_apply=%region_0.0 | all-reduce | flops 256 | bytes 2048 | tf_op jit(solution)/shard_map/psum | solution.py:55
  34.1 1.5 cholesky.74
  35.6 0.6 compare_reduce_fusion.3
  36.3 0.7 fusion.41
  36.9 1.2 custom-call.10
  38.2 0.3 convolution_bitcast_fusion.1
  38.5 0.6 copy.27
  39.2 10.4 %all-reduce.8.cloned.1.call-done = f32[32768]{0:T(1024)} async-done(((f32[32768]{0:T(1024)}), f32[32768]{0:T(1024)}) %all-reduce.8.cloned.1.call-update) | async-done | bytes 131088 | tf_op jit(solution)/shard_map/psum | solution.py:54
  49.6 0.9 add_rsqrt_fusion
  50.5 3.3 multiply_convert_fusion.1
  53.8 0.3 copy.25
  54.1 0.3 fusion.71
  54.4 1.2 fusion.6
  55.6 1.2 fusion.35
  56.8 1.6 copy.26
  58.5 57.0 %all-reduce.14.cloned.1.call-done = (f32[16,16384]{1,0:T(8,128)}, f32[16384]{0:T(1024)}) async-done(((f32[16,16384]{1,0:T(8,128)}, f32[16384]{0:T(1024)}), (f32[16,16384]{1,0:T(8,128)}, f32[16384]{0:T(1024)})) %all-reduce.14.cloned.1.call-update) | async-done | bytes 1114128 | tf_op jit(solution)/shard_map/psum | solution.py:89
  115.5 0.9 add_rsqrt_fusion.1
  116.3 3.0 convolution_multiply_fusion.2
  119.4 12.0 %psum.81 = f32[16,16]{1,0:T(8,128)S(1)} all-reduce(f32[16,16]{1,0:T(8,128)S(1)} %convolution_multiply_fusion.2), channel_id=1, replica_groups=mesh['doc'=4,'term'=8] {'doc'}, use_global_device_ids=true, to_apply=%region_6.9 | all-reduce | flops 256 | bytes 2048 | tf_op jit(solution)/shard_map/psum | solution.py:83
  131.5 1.5 cholesky.85
  133.0 0.6 compare_reduce_fusion.2
  133.7 0.6 fusion.59
  134.3 1.2 custom-call.11
  135.5 3.4 multiply_convert_fusion.2
  139.0 0.2 copy.28
  139.1 0.2 fusion.74
  139.4 0.6 fusion.2
  140.0 2.0 fusion.33
  142.1 2.5 copy.29
  144.7 0.7 constant_dynamic-update-slice_fusion.4
  145.3 82.1 %all-reduce.10.cloned.1.call-done = f32[16,32768]{1,0:T(8,128)} async-done(((f32[16,32768]{1,0:T(8,128)}), f32[16,32768]{1,0:T(8,128)}) %all-reduce.10.cloned.1.call-update) | async-done | bytes 2097168 | tf_op jit(solution)/shard_map/psum | solution.py:102
  227.5 5.2 %fusion.14 = f32[16,16]{1,0:T(8,128)S(1)} fusion(f32[16,32768]{1,0:T(8,128)} %all-reduce.10.cloned.1.call-done, f32[32768]{0:T(1024)S(1)} %add_rsqrt_fusion), kind=kOutput, calls=%fused_computation.20 | convolution fusion | flops 101187840 | bytes 2229248 | tf_op jit(solution)/shard_map/dot_general | solution.py:19
  232.7 4.4 %fusion.17 = f32[16,16]{1,0:T(8,128)S(1)} fusion(f32[16,32768]{1,0:T(8,128)S(1)} %copy-done.4, f32[16,32768]{1,0:T(8,128)} %all-reduce.10.cloned.1.call-done, f32[32768]{0:T(1024)S(1)} %add_rsqrt_fusion), kind=kOutput, calls=%fused_computation.27 | convolution fusion | flops 101187840 | bytes 4326400 | tf_op jit(solution)/shard_map/dot_general | solution.py:18
  237.1 23.7 %all-reduce = (f32[16,16]{1,0:T(8,128)S(1)}, f32[16,16]{1,0:T(8,128)S(1)}) all-reduce(f32[16,16]{1,0:T(8,128)S(1)} %fusion.17, f32[16,16]{1,0:T(8,128)S(1)} %fusion.14), channel_id=1, replica_groups=mesh['doc'=4,'term'=8] {'term'}, use_global_device_ids=true, to_apply=%region_9.0 | all-reduce | flops 512 | bytes 4096 | tf_op jit(solution)/shard_map/psum | solution.py:86
  261.1 1.5 cholesky.96
  262.6 0.6 compare_reduce_fusion.1
  263.2 0.6 fusion.58
  263.9 1.2 custom-call.12
  265.1 4.2 %convolution_subtract_fusion = f32[16,32768]{1,0:T(8,128)S(1)} fusion(f32[16,16]{1,0:T(8,128)S(1)} %get-tuple-element.6, f32[16,32768]{1,0:T(8,128)} %get-tuple-element.13, f32[16,32768]{1,0:T(8,128)} %all-reduce.10.cloned.1.call-done, f32[32768]{0:T(1024)S(1)} %add_rsqrt_fusion), kind=kOutput, calls=%fused_computation | convolution fusion | flops 101711872 | bytes 6423552 | tf_op jit(solution)/shard_map/dot_general | solution.py:23
  269.3 3.3 multiply_convert_fusion
  272.6 0.3 copy.30
  273.0 0.3 fusion.69
  273.3 1.2 fusion
  274.5 1.2 fusion.31
  275.6 1.6 copy.31
  277.2 1.9 constant_dynamic-slice_fusion
  279.1 0.6 constant_dynamic-update-slice_fusion.2
  279.8 51.9 %all-reduce.12.cloned.1.call-done = f32[16,16384]{1,0:T(8,128)} async-done(((f32[16,16384]{1,0:T(8,128)}), f32[16,16384]{1,0:T(8,128)}) %all-reduce.12.cloned.1.call-update) | async-done | bytes 1048592 | tf_op jit(solution)/shard_map/psum | solution.py:89
  331.7 3.1 convolution_multiply_fusion.1
  334.8 3.0 convolution_multiply_fusion
  337.9 18.7 %all-reduce.2 = (f32[16,16]{1,0:T(8,128)S(1)}, f32[16,16]{1,0:T(8,128)S(1)}) all-reduce(f32[16,16]{1,0:T(8,128)S(1)} %convolution_multiply_fusion, f32[16,16]{1,0:T(8,128)S(1)} %convolution_multiply_fusion.1), channel_id=1, replica_groups=mesh['doc'=4,'term'=8] {'doc'}, use_global_device_ids=true, to_apply=%region_12.16 | all-reduce | flops 512 | bytes 4096 | tf_op jit(solution)/shard_map/psum | solution.py:83
  356.8 1.5 cholesky.107
  358.3 0.6 compare_reduce_fusion
  359.0 0.6 select_bitcast_fusion
  359.6 1.2 custom-call.13
  360.8 0.7 constant_dynamic-update-slice_fusion
  361.5 2.2 convolution_subtract_fusion.1
  363.8 1.0 fusion.42
  364.8 0.7 constant_dynamic-slice_fusion.1
  (47 shorter events, 1.3 us)
Async XLA Ops:
  7.2 8.2 %copy-start = (f32[16,32768]{1,0:T(8,128)S(1)}, f32[16,32768]{1,0:T(8,128)}, u32[]{:S(2)}) copy-start(f32[16,32768]{1,0:T(8,128)} %param.14) | copy-start | bytes 6291460
  7.2 3.7 copy-start.6
  7.2 42.4 %all-reduce.8.cloned.1.call-start = ((), (), s32[]{:S(2)}) async-start(), calls=%async_computation | async-start | bytes 262144 | tf_op jit(solution)/shard_map/psum | solution.py:54
  12.0 103.5 %all-reduce.14.cloned.1.call-start = ((), (), s32[]{:S(2)}) async-start(), calls=%async_computation.3 | async-start | bytes 2228224 | tf_op jit(solution)/shard_map/psum | solution.py:89
  15.4 22.8 %copy-start.7 = (s32[1,1,8]{2,1,0:T(1,128)S(1)}, s32[1,1,8]{2,1,0:T(1,128)}, u32[]{:S(2)}) copy-start(s32[1,1,8]{2,1,0:T(1,128)} %param.11) | copy-start | bytes 100
  50.5 3.9 %copy-start.1 = (bf16[1,1,8,512,512]{4,3,2,1,0:T(8,128)(2,1)S(1)}, bf16[1,1,8,512,512]{4,3,2,1,0:T(8,128)(2,1)}, u32[]{:S(2)}) copy-start(bf16[1,1,8,512,512]{4,3,2,1,0:T(8,128)(2,1)} %param.10) | copy-start | bytes 12582916
  58.4 169.0 %all-reduce.10.cloned.1.call-start = ((), (), s32[]{:S(2)}) async-start(), calls=%async_computation.1 | async-start | bytes 4194304 | tf_op jit(solution)/shard_map/psum | solution.py:102
  135.5 3.8 %copy-start.2 = (bf16[1,1,8,512,512]{4,3,2,1,0:T(8,128)(2,1)S(1)}, bf16[1,1,8,512,512]{4,3,2,1,0:T(8,128)(2,1)}, u32[]{:S(2)}) copy-start(bf16[1,1,8,512,512]{4,3,2,1,0:T(8,128)(2,1)} %param.10) | copy-start | bytes 12582916
  144.6 187.1 %all-reduce.12.cloned.1.call-start = ((), (), s32[]{:S(2)}) async-start(), calls=%async_computation.2 | async-start | bytes 2097152 | tf_op jit(solution)/shard_map/psum | solution.py:89
  227.5 5.3 %copy-start.4 = (f32[16,32768]{1,0:T(8,128)S(1)}, f32[16,32768]{1,0:T(8,128)}, u32[]{:S(2)}) copy-start(f32[16,32768]{1,0:T(8,128)} %get-tuple-element.13) | copy-start | bytes 6291460
  269.3 3.9 %copy-start.3 = (bf16[1,1,8,512,512]{4,3,2,1,0:T(8,128)(2,1)S(1)}, bf16[1,1,8,512,512]{4,3,2,1,0:T(8,128)(2,1)}, u32[]{:S(2)}) copy-start(bf16[1,1,8,512,512]{4,3,2,1,0:T(8,128)(2,1)} %param.10) | copy-start | bytes 12582916
  331.7 29.8 %copy-start.5 = (f32[16,16384]{1,0:T(8,128)S(1)}, f32[16,16384]{1,0:T(8,128)}, u32[]{:S(2)}) copy-start(f32[16,16384]{1,0:T(8,128)} %all-reduce.12.cloned.1.call-done) | copy-start | bytes 3145732
  361.5 3.3 copy-start.8
Sparse Core Ops, SparseCore 0:
  12.1 37.3 all-reduce.7
  58.5 56.8 all-reduce.13
  144.8 82.6 all-reduce.9
  277.4 54.3 all-reduce.11
where the time goes:
time: 373 us; the launch traced here: 372 us
  waiting for transfers between devices  201 us (54%)
  blocking collectives  70.1 us (19%)
  matrix products  54.7 us (15%)
  other arithmetic  19.8 us (5%)
  between operations  14.7 us (4%)
  local copies, waits for them, and re-layouts  11 us (3%)
    psum x2, waiting for transfers between devices, doc_side(): return lax.psum(forward(right_block), 'term') * row_scale[None, :]  109 us
    psum x1, waiting for transfers between devices, on_device(): lax.psum(jnp.einsum('kc,kxb->xcb', col_live, product, precision=highest)....  82.1 us
    psum x2, blocking collectives, doc_total(): return lax.psum(partial_value, 'doc')  30.7 us
    psum x1, blocking collectives, term_total(): return lax.psum(partial_value, 'term')  23.7 us
    psum x1, blocking collectives, on_device(): lax.psum(jnp.dot(start_block, start_block.T, precision=highest) / n_terms...  15.8 us
    dot_general x3, matrix products, orthonormal(): jnp.dot(vectors, vectors.T, precision=highest) / total_rows  11.4 us
    psum x1, waiting for transfers between devices, on_device(): col_scale = lax.rsqrt(lax.psum(col_part, 'doc') + 1.0)  10.4 us
    unnamed x28, local copies, waits for them, and re-layouts  7.91 us
  transfers between devices with their start and end apart: 4, of which 4 were waited for; matrix products, arithmetic and copies ran while one was open for 4% of the time, Pallas kernels for 0%

commit v1 on v0

v1 whole, which is shorter than its diff:
```python
import functools

import jax
import jax.numpy as jnp
from jax import lax
from jax.experimental import pallas as pl
from jax.experimental.pallas import tpu as pltpu
from jax.sharding import PartitionSpec as P

TERM_TILES = 64
DOC_TILES = 32
LANES = 128
F32 = jnp.float32
BF16 = jnp.bfloat16
HIGHEST = lax.Precision.HIGHEST
VMEM = pltpu.MemorySpace.VMEM
SMEM = pltpu.MemorySpace.SMEM


def nn(a, b, precision=None):
    return lax.dot_general(
        a, b, (((1,), (0,)), ((), ())), precision=precision, preferred_element_type=F32
    )


def nt(a, b, precision=None):
    return lax.dot_general(
        a, b, (((1,), (1,)), ((), ())), precision=precision, preferred_element_type=F32
    )


def split2(x):
    high = x.astype(BF16)
    return jnp.concatenate([high, (x - high.astype(F32)).astype(BF16)], axis=0)


def split3(x):
    high = x.astype(BF16)
    rest = x - high.astype(F32)
    middle = rest.astype(BF16)
    low = (rest - middle.astype(F32)).astype(BF16)
    return jnp.concatenate([high, middle, low], axis=0)


def fold3(gram, edge):
    rows = gram[:edge] + gram[edge : 2 * edge] + gram[2 * edge :]
    return rows[:, :edge] + rows[:, edge : 2 * edge] + rows[:, 2 * edge :]


def pad_lanes(x):
    return jnp.concatenate([x, jnp.zeros((x.shape[0], LANES - x.shape[1]), F32)], axis=1)


def column_sums_body(cols, in_use, tile, start, sums, picked):
    slot = pl.program_id(0)
    edge = tile.shape[1]
    total = nn(jnp.ones((16, edge), BF16), tile[0])[0:1]
    live = slot < in_use[0]
    mark = jnp.where(live, cols[slot], -1).astype(F32)
    total = jnp.concatenate([jnp.where(live, total, 0.0), jnp.full((1, LANES), mark, F32)], axis=1)
    index = lax.broadcasted_iota(jnp.int32, sums.shape, 0)
    sums[...] = jnp.where(index == slot, total, sums[...])
    picked[0] = start[...]


def column_sums(tiles, start, cols, in_use):
    slots, edge, _ = tiles.shape
    vectors = start.shape[0]
    return pl.pallas_call(
        column_sums_body,
        grid_spec=pltpu.PrefetchScalarGridSpec(
            num_scalar_prefetch=2,
            grid=(slots,),
            in_specs=[
                pl.BlockSpec((1, edge, edge), lambda s, c, u: (s, 0, 0)),
                pl.BlockSpec((vectors, edge), lambda s, c, u: (0, c[s])),
            ],
            out_specs=[
                pl.BlockSpec((slots, edge + LANES), lambda s, c, u: (0, 0)),
                pl.BlockSpec((1, vectors, edge), lambda s, c, u: (s, 0, 0)),
            ],
        ),
        out_shape=[
            jax.ShapeDtypeStruct((slots, edge + LANES), F32),
            jax.ShapeDtypeStruct((slots, vectors, edge), F32),
        ],
        name="column_sums",
    )(cols, in_use, tiles, start)


def start_gram_body(start, gram, total):
    step = pl.program_id(0)
    vectors = start.shape[0]
    pieces = split3(start[...])
    part = nt(pieces, pieces)

    @pl.when(step == 0)
    def _():
        total[...] = part

    @pl.when(step > 0)
    def _():
        total[...] += part

    @pl.when(step == pl.num_programs(0) - 1)
    def _():
        gram[...] = pad_lanes(fold3(total[...], vectors))


def start_gram(start):
    vectors, count = start.shape
    chunk = count // 8
    return pl.pallas_call(
        start_gram_body,
        grid=(8,),
        in_specs=[pl.BlockSpec((vectors, chunk), lambda s: (0, s))],
        out_specs=pl.BlockSpec((vectors, LANES), lambda s: (0, 0)),
        out_shape=jax.ShapeDtypeStruct((vectors, LANES), F32),
        scratch_shapes=[pltpu.VMEM((3 * vectors, 3 * vectors), F32)],
        name="start_gram",
    )(start)


def first_forward_body(groups, *refs):
    rows, cols, in_use = refs[:3]
    tiles, picked, gram = refs[3:6]
    sums = refs[6 : 6 + groups]
    payload, col_scale = refs[6 + groups :]
    copies = payload.shape[0]
    slots, vectors, edge = picked.shape
    base = slots * vectors
    half = gram.shape[0] // 2
    values = [r[:, 0:edge] for r in sums]
    marks = [r[:, edge : edge + LANES] for r in sums]
    for s in range(slots):
        column = cols[s].astype(F32)
        degree = jnp.ones((1, edge), F32)
        for value, mark in zip(values, marks):
            same = jnp.where(mark == column, 1.0, 0.0)
            same = jnp.concatenate([same] * (edge // LANES), axis=1)
            degree = degree + jnp.sum(same * value, axis=0, keepdims=True)
        scale = lax.rsqrt(degree)
        col_scale[s : s + 1, :] = scale
        left = jnp.concatenate(
            [split2(picked[s] * scale), jnp.ones((vectors, edge), BF16)], axis=0
        )
        out = nt(left, tiles[s])
        product = out[:vectors] + out[vectors : 2 * vectors]
        for q in range(copies):
            payload[q, s * vectors : (s + 1) * vectors, :] = product
            payload[q, base + s : base + s + 1, :] = out[2 * vectors : 2 * vectors + 1]
        mark = jnp.where(s < in_use[0], rows[s], DOC_TILES).astype(F32)
        for q in range(copies):
            payload[q, base + slots + s : base + slots + s + 1, 2 * LANES : 3 * LANES] = jnp.full(
                (1, LANES), mark, F32
            )
    for q in range(copies):
        payload[q, base + slots : base + 2 * slots, 0:LANES] = gram[:half]
        payload[q, base + slots : base + 2 * slots, LANES : 2 * LANES] = gram[half:]
        payload[q, base + slots : base + 2 * slots, 3 * LANES :] = jnp.zeros(
            (slots, edge - 3 * LANES), F32
        )


def specs(*spaces):
    return [pl.BlockSpec(memory_space=space) for space in spaces]


def first_forward(copies, rows, cols, in_use, tiles, picked, gram, sums):
    slots, vectors, edge = picked.shape
    height = slots * vectors + 2 * slots
    return pl.pallas_call(
        functools.partial(first_forward_body, len(sums)),
        in_specs=specs(*[SMEM] * 3, *[VMEM] * (3 + len(sums))),
        out_specs=specs(VMEM, VMEM),
        out_shape=[
            jax.ShapeDtypeStruct((copies, height, edge), F32),
            jax.ShapeDtypeStruct((slots, edge), F32),
        ],
        name="first_forward",
    )(rows, cols, in_use, tiles, picked, gram, *sums)


def backward_body(
    rows, near, far, tiles, col_scale,
    dense, row_scale, low_half, high_half, gram, where, total, degree, marks, semaphores,
):
    members = near.shape[0]
    slots, edge = col_scale.shape
    vectors = dense.shape[1]
    base = slots * vectors
    tops = base + slots
    copies = [
        pltpu.make_async_copy(
            ref.at[:, tops : tops + slots, 2 * LANES : 3 * LANES], marks.at[p], semaphores.at[p]
        )
        for p, ref in enumerate((near, far))
    ]
    for copy in copies:
        copy.start()
    total[...] = jnp.zeros(total.shape, F32)
    degree[...] = jnp.ones(degree.shape, F32)
    first = jnp.zeros((slots, LANES), F32)
    second = jnp.zeros((slots, LANES), F32)
    for ref in (near, far):
        for d in range(members):
            first = first + ref[d, tops : tops + slots, 0:LANES]
            second = second + ref[d, tops : tops + slots, LANES : 2 * LANES]
    gram[0:slots, :] = first
    gram[slots : 2 * slots, :] = second
    for copy in copies:
        copy.wait()
    for p, ref in enumerate((near, far)):
        for d in range(members):
            for k in range(slots):
                row = marks[p, d, k, 0].astype(jnp.int32)
                where[(p * members + d) * slots + k] = row
                total[row] += ref[d, k * vectors : (k + 1) * vectors, :]
                degree[row] += ref[d, base + k : base + k + 1, :]
    degree[...] = lax.rsqrt(degree[...])
    for r in range(DOC_TILES):
        dense[r] = total[r] * degree[r]
    for s in range(slots):
        row = rows[s]
        scale = degree[row]
        row_scale[s : s + 1, :] = scale
        out = nn(split2(dense[row] * scale), tiles[s])
        product = (out[:vectors] + out[vectors:]) * col_scale[s : s + 1, :]
        if s < slots // 2:
            low_half[s * vectors : (s + 1) * vectors, :] = product
        else:
            t = s - slots // 2
            high_half[t * vectors : (t + 1) * vectors, :] = product


def backward(rows, near, far, tiles, col_scale):
    members = near.shape[0]
    slots, edge = col_scale.shape
    vectors = (near.shape[1] - 2 * slots) // slots
    half = jax.ShapeDtypeStruct((slots // 2 * vectors, edge), F32)
    return pl.pallas_call(
        backward_body,
        in_specs=specs(SMEM, *[VMEM] * 4),
        out_specs=specs(*[VMEM] * 5, SMEM),
        out_shape=[
            jax.ShapeDtypeStruct((DOC_TILES, vectors, edge), F32),
            jax.ShapeDtypeStruct((slots, edge), F32),
            half,
            half,
            jax.ShapeDtypeStruct((vectors, LANES), F32),
            jax.ShapeDtypeStruct((2 * members * slots,), jnp.int32),
        ],
        scratch_shapes=[
            pltpu.VMEM((DOC_TILES + 1, vectors, edge), F32),
            pltpu.VMEM((DOC_TILES + 1, 1, edge), F32),
            pltpu.SMEM((2, members, slots, LANES), F32),
            pltpu.SemaphoreType.DMA((2,)),
        ],
        name="backward",
    )(rows, near, far, tiles, col_scale)


def second_forward_body(groups, share, *refs):
    cols, place = refs[:2]
    tiles, col_scale, row_scale = refs[2:5]
    sums = refs[5 : 5 + groups]
    halves = refs[5 + groups : 5 + 3 * groups]
    payload, mine, total, marks, semaphores = refs[5 + 3 * groups :]
    slots, edge = col_scale.shape
    vectors = mine.shape[1]
    copies = [
        pltpu.make_async_copy(ref.at[:, edge : edge + LANES], marks.at[d], semaphores.at[d])
        for d, ref in enumerate(sums)
    ]
    for copy in copies:
        copy.start()
    total[...] = jnp.zeros(total.shape, F32)
    for copy in copies:
        copy.wait()
    for d in range(groups):
        for k in range(slots):
            mark = marks[d, k, 0].astype(jnp.int32)
            column = jnp.where(mark < 0, TERM_TILES, mark)
            part = halves[2 * d + k // (slots // 2)]
            t = k % (slots // 2)
            total[column] += part[t * vectors : (t + 1) * vectors, :]
    for s in range(slots):
        out = nt(split2(total[cols[s]] * col_scale[s : s + 1, :]), tiles[s])
        product = (out[:vectors] + out[vectors:]) * row_scale[s : s + 1, :]
        for q in range(payload.shape[0]):
            payload[q, s * vectors : (s + 1) * vectors, :] = product
    for t in range(share):
        mine[t] = total[place[0] * share + t]


def second_forward(copies, share, cols, place, tiles, col_scale, row_scale, sums, halves):
    slots, edge = col_scale.shape
    vectors = halves[0].shape[0] // (slots // 2)
    groups = len(sums)
    return pl.pallas_call(
        functools.partial(second_forward_body, groups, share),
        in_specs=specs(SMEM, SMEM, *[VMEM] * (3 + 3 * groups)),
        out_specs=specs(VMEM, VMEM),
        out_shape=[
            jax.ShapeDtypeStruct((copies, slots * vectors, edge), F32),
            jax.ShapeDtypeStruct((share, vectors, edge), F32),
        ],
        scratch_shapes=[
            pltpu.VMEM((TERM_TILES + 1, vectors, edge), F32),
            pltpu.SMEM((groups, slots, LANES), F32),
            pltpu.SemaphoreType.DMA((groups,)),
        ],
        name="second_forward",
    )(cols, place, tiles, col_scale, row_scale, *sums, *halves)


def document_gram_body(share, where, place, near, far, dense, gram, first, second, total):
    members = near.shape[0]
    _, vectors, edge = dense.shape
    slots = near.shape[1] // vectors
    total[...] = jnp.zeros(total.shape, F32)
    for p, ref in enumerate((near, far)):
        for d in range(members):
            for k in range(slots):
                row = where[(p * members + d) * slots + k]
                total[row] += ref[d, k * vectors : (k + 1) * vectors, :]
    out = jnp.zeros((6 * vectors, 6 * vectors), F32)
    for r in range(DOC_TILES):
        pieces = split3(jnp.concatenate([dense[r], total[r]], axis=0))
        out = out + nt(pieces, pieces)
    gram[...] = pad_lanes(fold3(out, 2 * vectors))
    for t in range(share):
        first[t] = dense[place[0] * share + t]
        second[t] = total[place[0] * share + t]


def document_gram(share, where, place, near, far, dense):
    _, vectors, edge = dense.shape
    piece = jax.ShapeDtypeStruct((share, vectors, edge), F32)
    return pl.pallas_call(
        functools.partial(document_gram_body, share),
        in_specs=specs(SMEM, SMEM, *[VMEM] * 3),
        out_specs=specs(*[VMEM] * 3),
        out_shape=[jax.ShapeDtypeStruct((2 * vectors, LANES), F32), piece, piece],
        scratch_shapes=[pltpu.VMEM((DOC_TILES + 1, vectors, edge), F32)],
        name="document_gram",
    )(where, place, near, far, dense)


def factorize(gram):
    edge = gram.shape[0]
    down = lax.broadcasted_iota(jnp.int32, (edge, edge), 0)
    across = lax.broadcasted_iota(jnp.int32, (edge, edge), 1)
    unit = jnp.where(down == across, 1.0, 0.0)
    work = jnp.concatenate([gram, unit], axis=1)
    index = lax.broadcasted_iota(jnp.int32, (edge, 2 * edge), 0)
    for k in range(edge):
        inverse = lax.rsqrt(work[k : k + 1, k : k + 1])
        pivot = work[k : k + 1, :] * inverse
        column = work[:, k : k + 1] * inverse
        work = jnp.where(
            index > k, work - column * pivot, jnp.where(index == k, pivot, work)
        )
    upper = jnp.where(down <= across, work[:, :edge], 0.0)
    lower = lax.dot_general(
        upper, unit, (((0,), (0,)), ((), ())), precision=HIGHEST, preferred_element_type=F32
    )
    return lower, upper, work[:, edge:]


def combine(factor, data):
    rows = factor.shape[0]
    out = nn(jnp.concatenate([split3(factor)] * 3, axis=1), split3(data))
    return out[:rows] + out[rows : 2 * rows] + out[2 * rows :]


def finish_body(groups, n_docs, n_terms, *refs):
    grams = refs[:groups]
    start_gram_ref, first, second, right_part, start = refs[groups : groups + 5]
    left_out, right_out, coefficients = refs[groups + 5 :]
    vectors = start.shape[0]
    edge = first.shape[2]
    gram = grams[0][...]
    for ref in grams[1:]:
        gram = gram + ref[...]
    low = gram[:vectors, :vectors]
    cross = gram[vectors:, :vectors]
    turned = gram[:vectors, vectors : 2 * vectors]
    high = gram[vectors:, vectors : 2 * vectors]
    mm = functools.partial(nn, precision=HIGHEST)
    mt = functools.partial(nt, precision=HIGHEST)
    _, _, inverse_zero = factorize(start_gram_ref[:, :vectors] / n_terms)
    lower_one, upper_one, inverse = factorize(mt(mm(inverse_zero, low / n_docs), inverse_zero))
    both = mm(inverse, inverse_zero)
    projection_one = upper_one * (n_docs / n_terms)
    sym = (cross + turned) * (0.5 / n_terms)
    lower_two, upper_two, inverse_two = factorize(
        mt(mm(both, sym), both) - mt(projection_one, projection_one)
    )
    projection_two = upper_two * (n_terms / n_docs)
    back = mm(projection_one, inverse_zero)
    right_factor = jnp.concatenate([mm(inverse_two, both), -mm(inverse_two, back)], axis=1)
    main = right_factor[:, :vectors]
    side = right_factor[:, vectors:] - mm(projection_two, both)
    main_high = mm(main, high) + mm(side, turned)
    main_low = mm(main, cross) + mm(side, low)
    lower_three, _, inverse_three = factorize(
        (mt(main_high, main) + mt(main_low, side)) / n_docs
    )
    left_factor = jnp.concatenate([mm(inverse_three, main), mm(inverse_three, side)], axis=1)
    for i, value in enumerate((lower_one, projection_one, lower_two, projection_two, lower_three)):
        coefficients[i] = value
    for t in range(right_part.shape[0]):
        data = jnp.concatenate([right_part[t], start[:, t * edge : (t + 1) * edge]], axis=0)
        right_out[:, t * edge : (t + 1) * edge] = combine(right_factor, data)
    for t in range(first.shape[0]):
        data = jnp.concatenate([second[t], first[t]], axis=0)
        left_out[:, t * edge : (t + 1) * edge] = combine(left_factor, data)


def finish(n_docs, n_terms, grams, gram_zero, first, second, right_part, start):
    vectors = start.shape[0]
    edge = first.shape[2]
    return pl.pallas_call(
        functools.partial(finish_body, len(grams), n_docs, n_terms),
        in_specs=specs(*[VMEM] * (len(grams) + 5)),
        out_specs=specs(*[VMEM] * 3),
        out_shape=[
            jax.ShapeDtypeStruct((vectors, first.shape[0] * edge), F32),
            jax.ShapeDtypeStruct((vectors, right_part.shape[0] * edge), F32),
            jax.ShapeDtypeStruct((5, vectors, vectors), F32),
        ],
        name="finish",
    )(*grams, gram_zero, first, second, right_part, start)


def shift(value, axis, step):
    size = lax.axis_size(axis)
    return lax.ppermute(value, axis, [(i, (i + step) % size) for i in range(size)])


def from_all(value, axis):
    return [value] + [shift(value, axis, k) for k in range(1, lax.axis_size(axis))]


def around(low, high, axis):
    size = lax.axis_size(axis)
    lows, highs = {0: low}, {0: high}
    ahead, behind = (low, high), (low, high)
    for k in range(1, size // 2 + 1):
        if 2 * k < size:
            ahead = (shift(ahead[0], axis, 1), shift(ahead[1], axis, 1))
            behind = (shift(behind[0], axis, -1), shift(behind[1], axis, -1))
            lows[k], highs[k] = ahead
            lows[size - k], highs[size - k] = behind
        else:
            lows[k] = shift(ahead[0], axis, 1)
            highs[k] = shift(behind[1], axis, -1)
    return [half for k in range(size) for half in (lows[k], highs[k])]


def term_gather(payload):
    size = lax.axis_size("term")
    near = lax.all_to_all(
        payload, "term", 0, 0,
        axis_index_groups=[list(range(0, size, 2)), list(range(1, size, 2))],
    )
    far = lax.ppermute(near, "term", [(i, i ^ 1) for i in range(size)])
    return near, far


def on_device(tiles, tile_rows, tile_cols, counts, start):
    tiles = tiles[0, 0]
    rows = tile_rows[0, 0]
    cols = tile_cols[0, 0]
    in_use = counts[0]
    doc_groups = lax.axis_size("doc")
    term_groups = lax.axis_size("term")
    edge = tiles.shape[1]
    n_docs = DOC_TILES * edge * doc_groups
    n_terms = TERM_TILES * edge * term_groups
    members = term_groups // 2
    row_share = DOC_TILES // term_groups
    col_share = TERM_TILES // doc_groups
    doc_place = lax.axis_index("doc").reshape(1)
    term_place = lax.axis_index("term").reshape(1)
    sums, picked = column_sums(tiles, start, cols, in_use)
    all_sums = from_all(sums, "doc")
    gram_zero = start_gram(start)
    payload, col_scale = first_forward(
        members, rows, cols, in_use, tiles, picked, gram_zero, all_sums
    )
    near, far = term_gather(payload)
    dense, row_scale, low_half, high_half, gram_zero, where = backward(
        rows, near, far, tiles, col_scale
    )
    halves = around(low_half, high_half, "doc")
    payload, right_part = second_forward(
        members, col_share, cols, doc_place, tiles, col_scale, row_scale, all_sums, halves
    )
    near, far = term_gather(payload)
    gram, first, second = document_gram(row_share, where, term_place, near, far, dense)
    mine = lax.dynamic_slice_in_dim(
        start, lax.axis_index("doc") * (col_share * edge), col_share * edge, 1
    )
    return finish(
        n_docs, n_terms, from_all(gram, "doc"), gram_zero, first, second, right_part, mine
    )


def solution(mesh):
    in_specs = (
        P("doc", "term", None, None, None),
        P("doc", "term", None),
        P("doc", "term", None),
        P("doc", "term"),
        P(None, "term"),
    )
    out_specs = (P(None, ("doc", "term")), P(None, ("term", "doc")), P())
    return jax.shard_map(
        on_device, mesh=mesh, in_specs=in_specs, out_specs=out_specs, check_vma=False
    )
```

time: 373 us -> 124 us (0.33)
  waiting for transfers between devices: 201 us -> 16.3 us
  matrix products: 54.7 us -> 0 us
  Pallas kernels: 0 us -> 42.8 us
  blocking collectives: 70.1 us -> 34.9 us
  starting transfers between devices: 0.16 us -> 22.5 us
  other arithmetic: 19.8 us -> 0 us
  between operations: 14.7 us -> 1.39 us
  local copies, waits for them, and re-layouts: 11 us -> 5.73 us
    psum x4 -> x0, waiting for transfers between devices: 201 us -> none  [the longest x2 109 us: doc_side(): return lax.psum(forward(right_block), 'term') * row_scale[None, :]]
    psum x4 -> x0, blocking collectives: 70.1 us -> none  [the longest x2 30.7 us: doc_total(): return lax.psum(partial_value, 'doc')]
    dot_general x23 -> x0, matrix products: 43.6 us -> none  [the longest x3 11.4 us: orthonormal(): jnp.dot(vectors, vectors.T, precision=highest) / total_rows]
    pallas_call x0 -> x7, Pallas kernels: none -> 42.8 us  [the longest x1 9.57 us: finish(): pl.pallas_call(functools.partial(finish_body, len(grams), n_docs, n_terms...]
    all_to_all x0 -> x2, blocking collectives: none -> 34.9 us  [term_gather(): lax.all_to_all(payload, 'term', 0, 0, axis_index_groups=[list(range(0, si...]
    ppermute x0 -> x14, starting transfers between devices: none -> 22.5 us  [the longest x12 22.5 us: shift(): lax.ppermute(value, axis, [(i, (i + step) % size) for i in range(size)])]
    another operation x21 -> x0, other arithmetic: 16.7 us -> none  [the longest x9 6.41 us: orthonormal(): factor = jnp.linalg.cholesky(gram_matrix)]
    ppermute x0 -> x14, waiting for transfers between devices: none -> 16.3 us  [the longest x12 10.8 us: shift(): lax.ppermute(value, axis, [(i, (i + step) % size) for i in range(size)])]
  transfers between devices with their start and end apart: 4 -> 14, of which waited for: 4 -> 8; matrix products, arithmetic and copies ran while one was open for 4% -> 2% of each run, Pallas kernels for 0% -> 5%
where the time goes in v1:
time: 124 us
  Pallas kernels  42.8 us (35%)
  blocking collectives  34.9 us (28%)
  starting transfers between devices  22.5 us (18%)
  waiting for transfers between devices  16.3 us (13%)
  local copies, waits for them, and re-layouts  5.73 us (5%)
  between operations  1.39 us (1%)
    all_to_all x2, blocking collectives, term_gather(): lax.all_to_all(payload, 'term', 0, 0, axis_index_groups=[list(range(0, si...  34.9 us
    ppermute x12, starting transfers between devices, shift(): lax.ppermute(value, axis, [(i, (i + step) % size) for i in range(size)])  22.5 us
    ppermute x12, waiting for transfers between devices, shift(): lax.ppermute(value, axis, [(i, (i + step) % size) for i in range(size)])  10.8 us
    pallas_call x1, Pallas kernels, finish(): pl.pallas_call(functools.partial(finish_body, len(grams), n_docs, n_terms...  9.57 us
    pallas_call x1, Pallas kernels, column_sums(): pl.pallas_call(column_sums_body, grid_spec=pltpu.PrefetchScalarGridSpec(n...  6.79 us
    pallas_call x1, Pallas kernels, second_forward(): pl.pallas_call(functools.partial(second_forward_body, groups, share), in_...  5.98 us
    pallas_call x1, Pallas kernels, backward(): pl.pallas_call(backward_body, in_specs=specs(SMEM, *[VMEM] * 4), out_spec...  5.96 us
    pallas_call x1, Pallas kernels, start_gram(): pl.pallas_call(start_gram_body, grid=(8,), in_specs=[pl.BlockSpec((vector...  5.88 us
  transfers between devices with their start and end apart: 14, of which 8 were waited for; matrix products, arithmetic and copies ran while one was open for 2% of the time, Pallas kernels for 5%

profile of v1, /device:TPU:0, one launch (start us, length us, event | category | flops | bytes accessed | tf_op | source)
XLA Modules:
  0.0 123.5 jit_solution(11700044953054083191)
XLA Ops:
  1.3 6.8 %column_sums.1 = (f32[8,640]{1,0:T(8,128)}, f32[8,16,512]{2,1,0:T(8,128)}) custom-call(s32[8]{0:T(128)} %bitcast.12, s32[1]{0:T(128)} %bitcast.6.in_use, bf16[8,512,512]{2,1,0:T(8,128)(2,1)} %bitcast.8, f32[16,32768]{1,0:T(8,128)} %start.3), custom_call_target="tpu_custom_call" | custom-call | tf_op jit(solution)/shard_map/column_sums/pallas_call | solution.py:69
  8.1 3.0 %collective-permute-start = (f32[8,640]{1,0:T(8,128)}, f32[8,640]{1,0:T(8,128)S(1)}, u32[]{:S(2)}, u32[]{:S(2)}) collective-permute-start(f32[8,640]{1,0:T(8,128)} %get-tuple-element.19.refs_6_.refs_5_), channel_id=1, source_target_pairs={{0,8},{8,16},{16,24},{24,0},{1,9},{9,17},{17,25},{25,1},{2,10},{10... | collective-permute-start | bytes 61448 | tf_op jit(solution)/shard_map/ppermute | solution.py:439
  11.1 2.6 %collective-permute-start.1 = (f32[8,640]{1,0:T(8,128)}, f32[8,640]{1,0:T(8,128)S(1)}, u32[]{:S(2)}, u32[]{:S(2)}) collective-permute-start(f32[8,640]{1,0:T(8,128)} %get-tuple-element.19.refs_6_.refs_5_), channel_id=1, source_target_pairs={{0,16},{8,24},{16,0},{24,8},{1,17},{9,25},{17,1},{25,9},{2,18},{10... | collective-permute-start | bytes 61448 | tf_op jit(solution)/shard_map/ppermute | solution.py:439
  13.7 1.3 %collective-permute-start.2 = (f32[8,640]{1,0:T(8,128)}, f32[8,640]{1,0:T(8,128)S(1)}, u32[]{:S(2)}, u32[]{:S(2)}) collective-permute-start(f32[8,640]{1,0:T(8,128)} %get-tuple-element.19.refs_6_.refs_5_), channel_id=1, source_target_pairs={{0,24},{8,0},{16,8},{24,16},{1,25},{9,1},{17,9},{25,17},{2,26},{10... | collective-permute-start | bytes 61448 | tf_op jit(solution)/shard_map/ppermute | solution.py:439
  15.1 5.9 %start_gram.1.refs_5_ = f32[16,128]{1,0:T(8,128)} custom-call(f32[16,32768]{1,0:T(8,128)} %start.3), custom_call_target="tpu_custom_call" | custom-call | tf_op jit(solution)/shard_map/start_gram/pallas_call | solution.py:113
  20.9 0.0 collective-permute-done.refs_7_.refs_6_
  20.9 0.0 copy-start.10
  20.9 0.0 collective-permute-done.1.refs_8_.refs_7_
  20.9 0.0 copy-start.11
  21.0 0.0 collective-permute-done.2.refs_9_.refs_8_
  21.0 0.0 copy-start.12
  21.0 0.6 copy-done.10
  21.5 0.0 copy-done.11
  21.6 0.0 copy-done.12
  21.6 4.7 %first_forward.1 = (f32[4,144,512]{2,1,0:T(8,128)}, f32[8,512]{1,0:T(8,128)}) custom-call(s32[8]{0:T(128)} %bitcast.15, s32[8]{0:T(128)} %bitcast.13, s32[1]{0:T(128)} %bitcast.7.refs_2_, bf16[8,512,512]{2,1,0:T(8,128)(2,1)} %bitcast.9, f32[8,16,512]{2,1,0:T(8,128)} %get-tuple-element.18.refs_4_, f32[16,128]{1,0:T(8,128)} %start_gram.1.refs_5_, ...), custom_call_target="tpu_custom_call" | custom-call | tf_op jit(solution)/shard_map/first_forward/pallas_call | solution.py:172
  26.3 18.5 %all_to_all.10.near = f32[4,144,512]{2,1,0:T(8,128)S(1)} all-to-all(f32[4,144,512]{2,1,0:T(8,128)} %get-tuple-element.20), channel_id=1, replica_groups={{0,2,4,6},{1,3,5,7},{8,10,12,14},{9,11,13,15},{16,18,20,22},{17,19,21,2..., dimensions={0} | all-to-all | bytes 2359296 | tf_op jit(solution)/shard_map/all_to_all | solution.py:464
  44.8 0.0 copy-start
  44.8 0.0 collective-permute-start.3
  44.8 2.8 %collective-permute-done.3.far = f32[4,144,512]{2,1,0:T(8,128)S(1)} collective-permute-done((f32[4,144,512]{2,1,0:T(8,128)S(1)}, f32[4,144,512]{2,1,0:T(8,128)S(1)}, u32[]{:S(2)}, u32[]{:S(2)}) %collective-permute-start.3) | collective-permute-done | bytes 1179680 | tf_op jit(solution)/shard_map/ppermute | solution.py:468
  47.6 0.0 copy-start.2
  47.6 0.0 copy-done
  47.6 1.0 copy-done.2
  48.7 6.0 %backward.1 = (f32[32,16,512]{2,1,0:T(8,128)}, f32[8,512]{1,0:T(8,128)}, f32[64,512]{1,0:T(8,128)}, f32[64,512]{1,0:T(8,128)}, f32[16,128]{1,0:T(8,128)}, /*index=5*/s32[64]{0:T(128)}) custom-call(s32[8]{0:T(128)} %bitcast.16, f32[4,144,512]{2,1,0:T(8,128)} %copy-done, f32[4,144,512]{2,1,0:T(8,128)} %copy-done.2, bf16[8,512,512]{2,1,0:T(8,128)(2,1)} %bitcast.10, ...), custom_call_target="tpu_custom_call" | custom-call | tf_op jit(solution)/shard_map/backward/pallas_call | solution.py:241
  54.6 0.7 collective-permute-start.4
  55.4 3.1 %collective-permute-start.7 = (f32[64,512]{1,0:T(8,128)}, f32[64,512]{1,0:T(8,128)S(1)}, u32[]{:S(2)}, u32[]{:S(2)}) collective-permute-start(f32[64,512]{1,0:T(8,128)} %get-tuple-element.25.refs_10_), channel_id=1, source_target_pairs={{0,24},{8,0},{16,8},{24,16},{1,25},{9,1},{17,9},{25,17},{2,26},{10... | collective-permute-start | bytes 393224 | tf_op jit(solution)/shard_map/ppermute | solution.py:439
  58.5 0.0 collective-permute-start.5
  58.5 3.8 %collective-permute-start.9 = (f32[64,512]{1,0:T(8,128)}, f32[64,512]{1,0:T(8,128)S(1)}, u32[]{:S(2)}, u32[]{:S(2)}) collective-permute-start(f32[64,512]{1,0:T(8,128)} %get-tuple-element.24.refs_9_), channel_id=1, source_target_pairs={{0,24},{8,0},{16,8},{24,16},{1,25},{9,1},{17,9},{25,17},{2,26},{10... | collective-permute-start | bytes 393224 | tf_op jit(solution)/shard_map/ppermute | solution.py:439
  62.3 0.8 collective-permute-done.4.refs_11_
  63.1 0.0 copy-start.4
  63.1 0.0 collective-permute-start.6
  63.1 2.1 %collective-permute-done.7.refs_16_ = f32[64,512]{1,0:T(8,128)S(1)} collective-permute-done((f32[64,512]{1,0:T(8,128)}, f32[64,512]{1,0:T(8,128)S(1)}, u32[]{:S(2)}, u32[]{:S(2)}) %collective-permute-start.7) | collective-permute-done | bytes 131104 | tf_op jit(solution)/shard_map/ppermute | solution.py:439
  65.2 0.0 copy-start.5
  65.2 1.7 %collective-permute-start.8 = (f32[64,512]{1,0:T(8,128)S(1)}, f32[64,512]{1,0:T(8,128)S(1)}, u32[]{:S(2)}, u32[]{:S(2)}) collective-permute-start(f32[64,512]{1,0:T(8,128)S(1)} %collective-permute-done.7.refs_16_), channel_id=1, source_target_pairs={{0,24},{8,0},{16,8},{24,16},{1,25},{9,1},{17,9},{25,17},{2,26},{10... | collective-permute-start | bytes 393224 | tf_op jit(solution)/shard_map/ppermute | solution.py:439
  67.0 1.8 %collective-permute-done.5.refs_12_ = f32[64,512]{1,0:T(8,128)S(1)} collective-permute-done((f32[64,512]{1,0:T(8,128)}, f32[64,512]{1,0:T(8,128)S(1)}, u32[]{:S(2)}, u32[]{:S(2)}) %collective-permute-start.5) | collective-permute-done | bytes 131104 | tf_op jit(solution)/shard_map/ppermute | solution.py:439
  68.8 0.0 copy-start.6
  68.8 2.0 %collective-permute-done.9.refs_15_ = f32[64,512]{1,0:T(8,128)S(1)} collective-permute-done((f32[64,512]{1,0:T(8,128)}, f32[64,512]{1,0:T(8,128)S(1)}, u32[]{:S(2)}, u32[]{:S(2)}) %collective-permute-start.9) | collective-permute-done | bytes 131104 | tf_op jit(solution)/shard_map/ppermute | solution.py:439
  70.8 3.6 %collective-permute-done.6.refs_13_ = f32[64,512]{1,0:T(8,128)S(1)} collective-permute-done((f32[64,512]{1,0:T(8,128)S(1)}, f32[64,512]{1,0:T(8,128)S(1)}, u32[]{:S(2)}, u32[]{:S(2)}) %collective-permute-start.6) | collective-permute-done | bytes 131104 | tf_op jit(solution)/shard_map/ppermute | solution.py:439
  74.4 0.4 collective-permute-done.8.refs_14_
  74.9 0.0 copy-done.4
  74.9 0.0 copy-done.5
  74.9 0.0 copy-done.6
  74.9 0.0 copy-done.7
  74.9 0.2 copy-done.8
  75.1 0.5 copy-done.9
  75.5 6.0 %second_forward.1 = (f32[4,128,512]{2,1,0:T(8,128)}, f32[16,16,512]{2,1,0:T(8,128)}) custom-call(s32[8]{0:T(128)} %bitcast.14, s32[1]{0:T(128)} %bitcast.5.refs_1_, bf16[8,512,512]{2,1,0:T(8,128)(2,1)} %bitcast.11, f32[8,512]{1,0:T(8,128)} %get-tuple-element.21.col_scale.refs_3_, f32[8,512]{1,0:T(8,128)} %get-tuple-element.23.refs_4_, ...), custom_call_target="tpu_custom_call" | custom-call | tf_op jit(solution)/shard_map/second_forward/pallas_call | solution.py:300
  81.5 16.4 %all_to_all.11.near = f32[4,128,512]{2,1,0:T(8,128)S(1)} all-to-all(f32[4,128,512]{2,1,0:T(8,128)} %get-tuple-element.26), channel_id=1, replica_groups={{0,2,4,6},{1,3,5,7},{8,10,12,14},{9,11,13,15},{16,18,20,22},{17,19,21,2..., dimensions={0} | all-to-all | bytes 2097152 | tf_op jit(solution)/shard_map/all_to_all | solution.py:464
  97.9 0.0 collective-permute-start.10
  97.9 2.7 %collective-permute-done.10.far = f32[4,128,512]{2,1,0:T(8,128)S(1)} collective-permute-done((f32[4,128,512]{2,1,0:T(8,128)S(1)}, f32[4,128,512]{2,1,0:T(8,128)S(1)}, u32[]{:S(2)}, u32[]{:S(2)}) %collective-permute-start.10) | collective-permute-done | bytes 1048608 | tf_op jit(solution)/shard_map/ppermute | solution.py:468
  100.6 0.0 copy-done.1
  100.6 1.0 copy-done.3
  101.5 3.9 %document_gram.1 = (f32[32,128]{1,0:T(8,128)}, f32[4,16,512]{2,1,0:T(8,128)}, f32[4,16,512]{2,1,0:T(8,128)}) custom-call(s32[64]{0:T(128)} %get-tuple-element.22.where, s32[1]{0:T(128)} %bitcast.4.place, f32[4,128,512]{2,1,0:T(8,128)} %copy-done.1, f32[4,128,512]{2,1,0:T(8,128)} %copy-done.3, f32[32,16,512]{2,1,0:T(8,128)} %get-tuple-element.27.dense), custom_call_target="tpu_custom_call" | custom-call | tf_op jit(solution)/shard_map/document_gram/pallas_call | solution.py:340
  105.4 0.0 collective-permute-start.11
  105.4 3.5 %collective-permute-start.12 = (f32[32,128]{1,0:T(8,128)}, f32[32,128]{1,0:T(8,128)S(1)}, u32[]{:S(2)}, u32[]{:S(2)}) collective-permute-start(f32[32,128]{1,0:T(8,128)} %get-tuple-element.28.refs_0_), channel_id=1, source_target_pairs={{0,16},{8,24},{16,0},{24,8},{1,17},{9,25},{17,1},{25,9},{2,18},{10... | collective-permute-start | bytes 49160 | tf_op jit(solution)/shard_map/ppermute | solution.py:439
  109.0 2.5 %collective-permute-start.13 = (f32[32,128]{1,0:T(8,128)}, f32[32,128]{1,0:T(8,128)S(1)}, u32[]{:S(2)}, u32[]{:S(2)}) collective-permute-start(f32[32,128]{1,0:T(8,128)} %get-tuple-element.28.refs_0_), channel_id=1, source_target_pairs={{0,24},{8,0},{16,8},{24,16},{1,25},{9,1},{17,9},{25,17},{2,26},{10... | collective-permute-start | bytes 49160 | tf_op jit(solution)/shard_map/ppermute | solution.py:439
  111.5 1.9 %constant_dynamic-slice_fusion.refs_8_ = f32[16,8192]{1,0:T(8,128)} fusion(f32[16,32768]{1,0:T(8,128)} %start.3, s32[]{:T(128)S(6)} %select_n.3), kind=kLoop, calls=%fused_computation | loop fusion | bytes 1048580 | tf_op jit(solution)/shard_map/dynamic_slice | solution.py:503
  113.3 0.0 collective-permute-done.11.refs_1_
  113.3 0.0 collective-permute-done.12.refs_2_
  113.4 0.0 copy-start.14
  113.4 0.0 collective-permute-done.13.refs_3_
  113.4 0.0 copy-start.15
  113.4 0.6 copy-done.13
  113.9 0.0 copy-done.14
  114.0 0.0 copy-done.15
  114.0 9.6 %finish.1 = (f32[16,2048]{1,0:T(8,128)}, f32[16,8192]{1,0:T(8,128)}, f32[5,16,16]{2,1,0:T(8,128)}) custom-call(f32[32,128]{1,0:T(8,128)} %get-tuple-element.28.refs_0_, f32[32,128]{1,0:T(8,128)} %copy-done.13, f32[32,128]{1,0:T(8,128)} %copy-done.14, f32[32,128]{1,0:T(8,128)} %copy-done.15, f32[16,128]{1,0:T(8,128)} %get-tuple-element.29.refs_4_, ...), custom_call_target="tpu_custom_call" | custom-call | tf_op jit(solution)/shard_map/finish/pallas_call | solution.py:424
  (6 shorter events, 0.0 us)
Async XLA Ops:
  8.1 12.9 %collective-permute-start = (f32[8,640]{1,0:T(8,128)}, f32[8,640]{1,0:T(8,128)S(1)}, u32[]{:S(2)}, u32[]{:S(2)}) collective-permute-start(f32[8,640]{1,0:T(8,128)} %get-tuple-element.19.refs_6_.refs_5_), channel_id=1, source_target_pairs={{0,8},{8,16},{16,24},{24,0},{1,9},{9,17},{17,25},{25,1},{2,10},{10... | collective-permute-start | bytes 61448 | tf_op jit(solution)/shard_map/ppermute | solution.py:439
  11.1 9.8 %collective-permute-start.1 = (f32[8,640]{1,0:T(8,128)}, f32[8,640]{1,0:T(8,128)S(1)}, u32[]{:S(2)}, u32[]{:S(2)}) collective-permute-start(f32[8,640]{1,0:T(8,128)} %get-tuple-element.19.refs_6_.refs_5_), channel_id=1, source_target_pairs={{0,16},{8,24},{16,0},{24,8},{1,17},{9,25},{17,1},{25,9},{2,18},{10... | collective-permute-start | bytes 61448 | tf_op jit(solution)/shard_map/ppermute | solution.py:439
  13.7 7.2 %collective-permute-start.2 = (f32[8,640]{1,0:T(8,128)}, f32[8,640]{1,0:T(8,128)S(1)}, u32[]{:S(2)}, u32[]{:S(2)}) collective-permute-start(f32[8,640]{1,0:T(8,128)} %get-tuple-element.19.refs_6_.refs_5_), channel_id=1, source_target_pairs={{0,24},{8,0},{16,8},{24,16},{1,25},{9,1},{17,9},{25,17},{2,26},{10... | collective-permute-start | bytes 61448 | tf_op jit(solution)/shard_map/ppermute | solution.py:439
  20.9 0.6 copy-start.10
  20.9 0.6 copy-start.11
  21.0 0.6 copy-start.12
  44.8 2.9 %copy-start = (f32[4,144,512]{2,1,0:T(8,128)}, f32[4,144,512]{2,1,0:T(8,128)S(1)}, u32[]{:S(2)}) copy-start(f32[4,144,512]{2,1,0:T(8,128)S(1)} %all_to_all.10.near) | copy-start | bytes 3538948
  44.8 2.8 %collective-permute-start.3 = (f32[4,144,512]{2,1,0:T(8,128)S(1)}, f32[4,144,512]{2,1,0:T(8,128)S(1)}, u32[]{:S(2)}, u32[]{:S(2)}) collective-permute-start(f32[4,144,512]{2,1,0:T(8,128)S(1)} %all_to_all.10.near), channel_id=1, source_target_pairs={{0,1},{1,0},{2,3},{3,2},{4,5},{5,4},{6,7},{7,6},{8,9},{9,8},{10,11... | collective-permute-start | bytes 3538952 | tf_op jit(solution)/shard_map/ppermute | solution.py:468
  47.6 1.0 copy-start.2
  54.6 8.5 %collective-permute-start.4 = (f32[64,512]{1,0:T(8,128)}, f32[64,512]{1,0:T(8,128)S(1)}, u32[]{:S(2)}, u32[]{:S(2)}) collective-permute-start(f32[64,512]{1,0:T(8,128)} %get-tuple-element.24.refs_9_), channel_id=1, source_target_pairs={{0,8},{8,16},{16,24},{24,0},{1,9},{9,17},{17,25},{25,1},{2,10},{10... | collective-permute-start | bytes 393224 | tf_op jit(solution)/shard_map/ppermute | solution.py:439
  55.4 9.9 %collective-permute-start.7 = (f32[64,512]{1,0:T(8,128)}, f32[64,512]{1,0:T(8,128)S(1)}, u32[]{:S(2)}, u32[]{:S(2)}) collective-permute-start(f32[64,512]{1,0:T(8,128)} %get-tuple-element.25.refs_10_), channel_id=1, source_target_pairs={{0,24},{8,0},{16,8},{24,16},{1,25},{9,1},{17,9},{25,17},{2,26},{10... | collective-permute-start | bytes 393224 | tf_op jit(solution)/shard_map/ppermute | solution.py:439
  58.5 10.3 %collective-permute-start.5 = (f32[64,512]{1,0:T(8,128)}, f32[64,512]{1,0:T(8,128)S(1)}, u32[]{:S(2)}, u32[]{:S(2)}) collective-permute-start(f32[64,512]{1,0:T(8,128)} %get-tuple-element.25.refs_10_), channel_id=1, source_target_pairs={{0,8},{8,16},{16,24},{24,0},{1,9},{9,17},{17,25},{25,1},{2,10},{10... | collective-permute-start | bytes 393224 | tf_op jit(solution)/shard_map/ppermute | solution.py:439
  58.5 12.3 %collective-permute-start.9 = (f32[64,512]{1,0:T(8,128)}, f32[64,512]{1,0:T(8,128)S(1)}, u32[]{:S(2)}, u32[]{:S(2)}) collective-permute-start(f32[64,512]{1,0:T(8,128)} %get-tuple-element.24.refs_9_), channel_id=1, source_target_pairs={{0,24},{8,0},{16,8},{24,16},{1,25},{9,1},{17,9},{25,17},{2,26},{10... | collective-permute-start | bytes 393224 | tf_op jit(solution)/shard_map/ppermute | solution.py:439
  63.1 11.8 %copy-start.4 = (f32[64,512]{1,0:T(8,128)}, f32[64,512]{1,0:T(8,128)S(1)}, u32[]{:S(2)}) copy-start(f32[64,512]{1,0:T(8,128)S(1)} %collective-permute-done.4.refs_11_) | copy-start | bytes 393220
  63.1 11.3 %collective-permute-start.6 = (f32[64,512]{1,0:T(8,128)S(1)}, f32[64,512]{1,0:T(8,128)S(1)}, u32[]{:S(2)}, u32[]{:S(2)}) collective-permute-start(f32[64,512]{1,0:T(8,128)S(1)} %collective-permute-done.4.refs_11_), channel_id=1, source_target_pairs={{0,8},{8,16},{16,24},{24,0},{1,9},{9,17},{17,25},{25,1},{2,10},{10... | collective-permute-start | bytes 393224 | tf_op jit(solution)/shard_map/ppermute | solution.py:439
  65.2 9.6 %copy-start.5 = (f32[64,512]{1,0:T(8,128)}, f32[64,512]{1,0:T(8,128)S(1)}, u32[]{:S(2)}) copy-start(f32[64,512]{1,0:T(8,128)S(1)} %collective-permute-done.7.refs_16_) | copy-start | bytes 393220
  65.2 9.6 %collective-permute-start.8 = (f32[64,512]{1,0:T(8,128)S(1)}, f32[64,512]{1,0:T(8,128)S(1)}, u32[]{:S(2)}, u32[]{:S(2)}) collective-permute-start(f32[64,512]{1,0:T(8,128)S(1)} %collective-permute-done.7.refs_16_), channel_id=1, source_target_pairs={{0,24},{8,0},{16,8},{24,16},{1,25},{9,1},{17,9},{25,17},{2,26},{10... | collective-permute-start | bytes 393224 | tf_op jit(solution)/shard_map/ppermute | solution.py:439
  68.8 6.1 %copy-start.6 = (f32[64,512]{1,0:T(8,128)}, f32[64,512]{1,0:T(8,128)S(1)}, u32[]{:S(2)}) copy-start(f32[64,512]{1,0:T(8,128)S(1)} %collective-permute-done.5.refs_12_) | copy-start | bytes 393220
  70.8 4.1 %copy-start.7 = (f32[64,512]{1,0:T(8,128)}, f32[64,512]{1,0:T(8,128)S(1)}, u32[]{:S(2)}) copy-start(f32[64,512]{1,0:T(8,128)S(1)} %collective-permute-done.9.refs_15_) | copy-start | bytes 393220
  74.4 0.6 copy-start.8
  74.9 0.7 copy-start.9
  97.9 2.7 %copy-start.1 = (f32[4,128,512]{2,1,0:T(8,128)}, f32[4,128,512]{2,1,0:T(8,128)S(1)}, u32[]{:S(2)}) copy-start(f32[4,128,512]{2,1,0:T(8,128)S(1)} %all_to_all.11.near) | copy-start | bytes 3145732
  97.9 2.7 %collective-permute-start.10 = (f32[4,128,512]{2,1,0:T(8,128)S(1)}, f32[4,128,512]{2,1,0:T(8,128)S(1)}, u32[]{:S(2)}, u32[]{:S(2)}) collective-permute-start(f32[4,128,512]{2,1,0:T(8,128)S(1)} %all_to_all.11.near), channel_id=1, source_target_pairs={{0,1},{1,0},{2,3},{3,2},{4,5},{5,4},{6,7},{7,6},{8,9},{9,8},{10,11... | collective-permute-start | bytes 3145736 | tf_op jit(solution)/shard_map/ppermute | solution.py:468
  100.6 1.0 copy-start.3
  105.4 7.9 %collective-permute-start.11 = (f32[32,128]{1,0:T(8,128)}, f32[32,128]{1,0:T(8,128)S(1)}, u32[]{:S(2)}, u32[]{:S(2)}) collective-permute-start(f32[32,128]{1,0:T(8,128)} %get-tuple-element.28.refs_0_), channel_id=1, source_target_pairs={{0,8},{8,16},{16,24},{24,0},{1,9},{9,17},{17,25},{25,1},{2,10},{10... | collective-permute-start | bytes 49160 | tf_op jit(solution)/shard_map/ppermute | solution.py:439
  105.4 7.9 %collective-permute-start.12 = (f32[32,128]{1,0:T(8,128)}, f32[32,128]{1,0:T(8,128)S(1)}, u32[]{:S(2)}, u32[]{:S(2)}) collective-permute-start(f32[32,128]{1,0:T(8,128)} %get-tuple-element.28.refs_0_), channel_id=1, source_target_pairs={{0,16},{8,24},{16,0},{24,8},{1,17},{9,25},{17,1},{25,9},{2,18},{10... | collective-permute-start | bytes 49160 | tf_op jit(solution)/shard_map/ppermute | solution.py:439
  109.0 4.4 %collective-permute-start.13 = (f32[32,128]{1,0:T(8,128)}, f32[32,128]{1,0:T(8,128)S(1)}, u32[]{:S(2)}, u32[]{:S(2)}) collective-permute-start(f32[32,128]{1,0:T(8,128)} %get-tuple-element.28.refs_0_), channel_id=1, source_target_pairs={{0,24},{8,0},{16,8},{24,16},{1,25},{9,1},{17,9},{25,17},{2,26},{10... | collective-permute-start | bytes 49160 | tf_op jit(solution)/shard_map/ppermute | solution.py:439
  113.3 0.6 copy-start.13
  113.4 0.6 copy-start.14
  113.4 0.6 copy-start.15
